TPU v7x, 128 devices: a whole 4x4x4 slice. The times are simulated.
128 devices in a mesh: row: 8 (over z, y_hi), col: 16 (over x, y_lo, core).
Axes of the slice: x: 4, y: 4 (y_hi: 2, y_lo: 2; y = y_hi * 2 + y_lo), z: 4, core: 2. Of those that a mesh axis runs over, the one named last changes fastest.
Arguments:
- tri_panels: float32 [8192, 8192], P('row', 'col'), may hold values from -1 to 2, as said below
- rhs_rows: float32 [8192, 2048], P(('row', 'col')), may hold values from -6 to 6
Outputs:
- rhs_grid: float32 [8192, 2048], P('row', 'col')
Inputs may be any that keep to these rules, and one draw needn't show every extreme that they name: `tri_panels`: in L's row order the entries above the diagonal are zero and the diagonal entries are positive.
All inputs are finite; a program needn't handle non-finite values.
Results may differ from a plain program's by a relative error of at most 0.00011.
Values sent between devices are 32-bit elements; how exact they have to be, the bound alone decides.
A program may use at most 256 MiB of HBM per device.

v0:
```python
import jax
import jax.numpy as jnp
from jax import lax
from jax.sharding import PartitionSpec as P


def picked(array, axis, root):
    return lax.dynamic_index_in_dim(lax.all_gather(array, axis), root, 0, keepdims=False)


def on_device(tri_panels, rhs_rows):
    row_count = lax.axis_size("row")
    col_count = lax.axis_size("col")
    row_position = lax.axis_index("row")
    col_position = lax.axis_index("col")
    local_rows, block_size = tri_panels.shape
    blocks = local_rows // block_size
    sub_rows = block_size // col_count
    parted = rhs_rows.reshape(blocks, sub_rows, rhs_rows.shape[1])
    state_rhs = lax.all_to_all(parted, "col", split_axis=2, concat_axis=1, tiled=True)
    identity_block = jnp.eye(block_size, dtype=jnp.float32)
    own_pieces = tri_panels.reshape(blocks, block_size, block_size)
    own_diag = lax.dynamic_index_in_dim(own_pieces, col_position // row_count, 0, keepdims=False)
    own_diag = jnp.where(col_position % row_count == row_position, own_diag, identity_block)
    own_inverse = jax.scipy.linalg.solve_triangular(own_diag, identity_block, lower=True)

    def advance(state_rhs, panel_cols, inverse_block, step_index, first_slot):
        count = blocks - first_slot
        owner_row = step_index % row_count
        slot_index = step_index // row_count
        pieces = panel_cols.reshape(count, block_size, block_size)
        current = lax.dynamic_index_in_dim(state_rhs, slot_index, 0, keepdims=False)
        local_solution = jnp.dot(
            inverse_block,
            current,
            precision=lax.Precision.HIGHEST,
            preferred_element_type=jnp.float32,
        )
        solution = picked(local_solution, "row", owner_row)
        stored = jnp.where(row_position == owner_row, solution, current)
        state_rhs = lax.dynamic_update_index_in_dim(state_rhs, stored, slot_index, 0)
        global_block = (first_slot + jnp.arange(count, dtype=jnp.int32)) * row_count + row_position
        product = jnp.einsum("sij,jc->sic", pieces, solution, precision=lax.Precision.HIGHEST)
        trailing = state_rhs[first_slot:]
        trailing = jnp.where(
            (global_block > step_index)[:, None, None], trailing - product, trailing
        )
        if first_slot > 0:
            return jnp.concatenate([state_rhs[:first_slot], trailing], 0)
        return trailing

    group_count = (col_count + row_count - 1) // row_count
    everything, inverses = (
        lax.all_gather(tri_panels, "col", axis=1, tiled=True),
        lax.all_gather(own_inverse, "col", axis=1, tiled=True),
    )
    for first_slot in range(group_count):
        begin_step = first_slot * row_count
        end_step = min(begin_step + row_count, col_count)
        own_rows = everything[first_slot * block_size :]

        def upfront_step(step_index, state_rhs, own_rows=own_rows, first_slot=first_slot):
            panel_cols = lax.dynamic_slice_in_dim(own_rows, step_index * block_size, block_size, 1)
            inverse_block = lax.dynamic_slice_in_dim(
                inverses, step_index * block_size, block_size, 1
            )
            return advance(state_rhs, panel_cols, inverse_block, step_index, first_slot)

        state_rhs = lax.fori_loop(begin_step, end_step, upfront_step, state_rhs)
    return state_rhs.reshape(local_rows, state_rhs.shape[2])


def solution(mesh):
    return jax.shard_map(
        on_device,
        mesh=mesh,
        in_specs=(P("row", "col"), P(("row", "col"), None)),
        out_specs=P("row", "col"),
        check_vma=False,
    )
```

profile of v0, /device:TPU:0, one launch (start us, length us, event | category | flops | bytes accessed | tf_op | source)
XLA Modules:
  0.0 1225.2 jit_solution(3915089604845928567)
XLA Ops:
  9.3 11.6 while.33
  20.9 39.3 %custom-call.4 = f32[4,128,128]{1,2,0:T(8,128)S(1)} custom-call(f32[4,128,128]{2,1,0:T(8,128)S(1)} %get-tuple-element.290), custom_call_target="InvertDiagBlocksLowerTriangular" | custom-call | tf_op jit(solution)/shard_map/jit(_solve_triangular)/triangular_solve | solution.py:25
  71.1 5.6 all-to-all-start
  76.7 14.4 %all-to-all-done = f32[16,1,8192]{2,1,0:T(1,128)S(1)} async-done(((f32[16,1,8192]{2,1,0:T(1,128)}), f32[16,1,8192]{2,1,0:T(1,128)S(1)}, u32[]{:S(2)}, u32[]{:S(2)}) %all-to-all-start) | async-done | bytes 524320 | tf_op jit(solution)/shard_map/all_to_all | solution.py:20
  96.2 91.5 %all-gather.13.cloned.1.call-done = f32[1024,8192]{1,0:T(8,128)} async-done(((f32[1024,512]{1,0:T(8,128)}), f32[1024,8192]{1,0:T(8,128)}) %all-gather.13.cloned.1.call-update) | async-done | bytes 33554448 | tf_op jit(solution)/shard_map/all_gather | solution.py:54
  187.7 11.5 slice.70
  199.2 82.4 %all-gather.11.cloned.1.call-done = f32[512,8192]{1,0:T(8,128)} async-done(((f32[512,512]{1,0:T(8,128)}), f32[512,8192]{1,0:T(8,128)}) %all-gather.11.cloned.1.call-update) | async-done | bytes 16777232 | tf_op jit(solution)/shard_map/all_gather | solution.py:55
  281.6 471.9 %while.31 = (s32[]{:T(128)}, f32[2,512,128]{2,1,0:T(8,128)S(1)}, s32[]{:T(128)}, f32[512,8192]{1,0:T(8,128)}, f32[1024,8192]{1,0:T(8,128)}, /*index=5*/s32[]{:T(...) while((s32[]{:T(128)}, f32[2,512,128]{2,1,0:T(8,128)S(1)}, ...), condition=%wide.region_1.2_spmd, body=%wide.region_0.1_spmd.sunk | while | flops 1208287232 | bytes 17039816 | solution.py:69
  286.3 53.0 %all-gather.15.cloned.1.call-done = f32[4096,128]{1,0:T(8,128)} async-done(((f32[512,128]{1,0:T(8,128)}), f32[4096,128]{1,0:T(8,128)}) %all-gather.15.cloned.1.call-update) | async-done | bytes 2097168 | tf_op jit(solution)/shard_map/while/body/eval_jaxpr/all_gather | solution.py:8
  340.3 3.0 fusion.64
  343.3 2.9 fusion.63
  348.1 49.8 %all-gather.15.cloned.1.call-done = f32[4096,128]{1,0:T(8,128)} async-done(((f32[512,128]{1,0:T(8,128)}), f32[4096,128]{1,0:T(8,128)}) %all-gather.15.cloned.1.call-update) | async-done | bytes 2097168 | tf_op jit(solution)/shard_map/while/body/eval_jaxpr/all_gather | solution.py:8
  398.9 3.0 fusion.64
  401.9 2.9 fusion.63
  406.7 49.8 %all-gather.15.cloned.1.call-done = f32[4096,128]{1,0:T(8,128)} async-done(((f32[512,128]{1,0:T(8,128)}), f32[4096,128]{1,0:T(8,128)}) %all-gather.15.cloned.1.call-update) | async-done | bytes 2097168 | tf_op jit(solution)/shard_map/while/body/eval_jaxpr/all_gather | solution.py:8
  457.5 3.0 fusion.64
  460.5 2.9 fusion.63
  465.3 49.8 %all-gather.15.cloned.1.call-done = f32[4096,128]{1,0:T(8,128)} async-done(((f32[512,128]{1,0:T(8,128)}), f32[4096,128]{1,0:T(8,128)}) %all-gather.15.cloned.1.call-update) | async-done | bytes 2097168 | tf_op jit(solution)/shard_map/while/body/eval_jaxpr/all_gather | solution.py:8
  516.1 3.0 fusion.64
  519.1 2.9 fusion.63
  523.9 49.8 %all-gather.15.cloned.1.call-done = f32[4096,128]{1,0:T(8,128)} async-done(((f32[512,128]{1,0:T(8,128)}), f32[4096,128]{1,0:T(8,128)}) %all-gather.15.cloned.1.call-update) | async-done | bytes 2097168 | tf_op jit(solution)/shard_map/while/body/eval_jaxpr/all_gather | solution.py:8
  574.7 3.0 fusion.64
  577.8 2.9 fusion.63
  582.5 49.8 %all-gather.15.cloned.1.call-done = f32[4096,128]{1,0:T(8,128)} async-done(((f32[512,128]{1,0:T(8,128)}), f32[4096,128]{1,0:T(8,128)}) %all-gather.15.cloned.1.call-update) | async-done | bytes 2097168 | tf_op jit(solution)/shard_map/while/body/eval_jaxpr/all_gather | solution.py:8
  633.3 3.0 fusion.64
  636.4 2.9 fusion.63
  641.1 49.8 %all-gather.15.cloned.1.call-done = f32[4096,128]{1,0:T(8,128)} async-done(((f32[512,128]{1,0:T(8,128)}), f32[4096,128]{1,0:T(8,128)}) %all-gather.15.cloned.1.call-update) | async-done | bytes 2097168 | tf_op jit(solution)/shard_map/while/body/eval_jaxpr/all_gather | solution.py:8
  692.0 3.0 fusion.64
  695.0 2.9 fusion.63
  699.8 49.8 %all-gather.15.cloned.1.call-done = f32[4096,128]{1,0:T(8,128)} async-done(((f32[512,128]{1,0:T(8,128)}), f32[4096,128]{1,0:T(8,128)}) %all-gather.15.cloned.1.call-update) | async-done | bytes 2097168 | tf_op jit(solution)/shard_map/while/body/eval_jaxpr/all_gather | solution.py:8
  750.6 3.0 fusion.64
  753.5 464.0 %while.32 = (s32[]{:T(128)}, f32[2,512,128]{2,1,0:T(8,128)S(1)}, s32[]{:T(128)}, f32[512,8192]{1,0:T(8,128)}, s32[1]{0:T(128)}, /*index=5*/f32[512,8192]{1,0:T(8...) while((s32[]{:T(128)}, f32[2,512,128]{2,1,0:T(8,128)S(1)}, ...), condition=%wide.region_3.4_spmd, body=%wide.region_2.3_spmd.sunk | while | flops 805634048 | bytes 12846105 | solution.py:69
  753.6 2.9 fusion.69
  756.6 51.6 %all-gather.17.cloned.1.call-done = f32[4096,128]{1,0:T(8,128)} async-done(((f32[512,128]{1,0:T(8,128)}), f32[4096,128]{1,0:T(8,128)}) %all-gather.17.cloned.1.call-update) | async-done | bytes 2097168 | tf_op jit(solution)/shard_map/while/body/eval_jaxpr/all_gather | solution.py:8
  811.6 2.9 fusion.69
  814.6 51.6 %all-gather.17.cloned.1.call-done = f32[4096,128]{1,0:T(8,128)} async-done(((f32[512,128]{1,0:T(8,128)}), f32[4096,128]{1,0:T(8,128)}) %all-gather.17.cloned.1.call-update) | async-done | bytes 2097168 | tf_op jit(solution)/shard_map/while/body/eval_jaxpr/all_gather | solution.py:8
  869.6 2.9 fusion.69
  872.6 51.6 %all-gather.17.cloned.1.call-done = f32[4096,128]{1,0:T(8,128)} async-done(((f32[512,128]{1,0:T(8,128)}), f32[4096,128]{1,0:T(8,128)}) %all-gather.17.cloned.1.call-update) | async-done | bytes 2097168 | tf_op jit(solution)/shard_map/while/body/eval_jaxpr/all_gather | solution.py:8
  927.6 2.9 fusion.69
  930.6 51.6 %all-gather.17.cloned.1.call-done = f32[4096,128]{1,0:T(8,128)} async-done(((f32[512,128]{1,0:T(8,128)}), f32[4096,128]{1,0:T(8,128)}) %all-gather.17.cloned.1.call-update) | async-done | bytes 2097168 | tf_op jit(solution)/shard_map/while/body/eval_jaxpr/all_gather | solution.py:8
  985.6 2.9 fusion.69
  988.6 51.6 %all-gather.17.cloned.1.call-done = f32[4096,128]{1,0:T(8,128)} async-done(((f32[512,128]{1,0:T(8,128)}), f32[4096,128]{1,0:T(8,128)}) %all-gather.17.cloned.1.call-update) | async-done | bytes 2097168 | tf_op jit(solution)/shard_map/while/body/eval_jaxpr/all_gather | solution.py:8
  1043.6 2.9 fusion.69
  1046.6 51.6 %all-gather.17.cloned.1.call-done = f32[4096,128]{1,0:T(8,128)} async-done(((f32[512,128]{1,0:T(8,128)}), f32[4096,128]{1,0:T(8,128)}) %all-gather.17.cloned.1.call-update) | async-done | bytes 2097168 | tf_op jit(solution)/shard_map/while/body/eval_jaxpr/all_gather | solution.py:8
  1101.6 2.9 fusion.69
  1104.6 51.6 %all-gather.17.cloned.1.call-done = f32[4096,128]{1,0:T(8,128)} async-done(((f32[512,128]{1,0:T(8,128)}), f32[4096,128]{1,0:T(8,128)}) %all-gather.17.cloned.1.call-update) | async-done | bytes 2097168 | tf_op jit(solution)/shard_map/while/body/eval_jaxpr/all_gather | solution.py:8
  1159.6 2.9 fusion.69
  1162.6 51.6 %all-gather.17.cloned.1.call-done = f32[4096,128]{1,0:T(8,128)} async-done(((f32[512,128]{1,0:T(8,128)}), f32[4096,128]{1,0:T(8,128)}) %all-gather.17.cloned.1.call-update) | async-done | bytes 2097168 | tf_op jit(solution)/shard_map/while/body/eval_jaxpr/all_gather | solution.py:8
  (131 shorter events, 83.3 us)
Async XLA Ops:
  6.5 1.6 copy-start.1
  6.5 181.1 %all-gather.13.cloned.1.call-start = ((), (), s32[]{:S(2)}) async-start(), calls=%async_computation.2 | async-start | bytes 35651584 | tf_op jit(solution)/shard_map/all_gather | solution.py:54
  7.3 274.3 %all-gather.11.cloned.1.call-start = ((), (), s32[]{:S(2)}) async-start(), calls=%async_computation.1 | async-start | bytes 17825792 | tf_op jit(solution)/shard_map/all_gather | solution.py:55
  65.7 1.5 copy-start.2
  71.1 20.0 %all-to-all-start = ((f32[16,1,8192]{2,1,0:T(1,128)}), f32[16,1,8192]{2,1,0:T(1,128)S(1)}, u32[]{:S(2)}, u32[]{:S(2)}) async-start(f32[16,1,8192]{2,1,0:T(1,128)} %reshape.83), calls=%async_computation | async-start | bytes 1048576 | tf_op jit(solution)/shard_map/all_to_all | solution.py:20
  281.6 57.7 %all-gather.15.cloned.1.call-start = ((), (), s32[]{:S(2)}) async-start(), calls=%async_computation.3 | async-start | bytes 2359296 | tf_op jit(solution)/shard_map/while/body/eval_jaxpr/all_gather | solution.py:8
  343.3 54.6 %all-gather.15.cloned.1.call-start = ((), (), s32[]{:S(2)}) async-start(), calls=%async_computation.3 | async-start | bytes 2359296 | tf_op jit(solution)/shard_map/while/body/eval_jaxpr/all_gather | solution.py:8
  401.9 54.6 %all-gather.15.cloned.1.call-start = ((), (), s32[]{:S(2)}) async-start(), calls=%async_computation.3 | async-start | bytes 2359296 | tf_op jit(solution)/shard_map/while/body/eval_jaxpr/all_gather | solution.py:8
  460.5 54.6 %all-gather.15.cloned.1.call-start = ((), (), s32[]{:S(2)}) async-start(), calls=%async_computation.3 | async-start | bytes 2359296 | tf_op jit(solution)/shard_map/while/body/eval_jaxpr/all_gather | solution.py:8
  519.1 54.7 %all-gather.15.cloned.1.call-start = ((), (), s32[]{:S(2)}) async-start(), calls=%async_computation.3 | async-start | bytes 2359296 | tf_op jit(solution)/shard_map/while/body/eval_jaxpr/all_gather | solution.py:8
  577.7 54.6 %all-gather.15.cloned.1.call-start = ((), (), s32[]{:S(2)}) async-start(), calls=%async_computation.3 | async-start | bytes 2359296 | tf_op jit(solution)/shard_map/while/body/eval_jaxpr/all_gather | solution.py:8
  636.3 54.6 %all-gather.15.cloned.1.call-start = ((), (), s32[]{:S(2)}) async-start(), calls=%async_computation.3 | async-start | bytes 2359296 | tf_op jit(solution)/shard_map/while/body/eval_jaxpr/all_gather | solution.py:8
  694.9 54.6 %all-gather.15.cloned.1.call-start = ((), (), s32[]{:S(2)}) async-start(), calls=%async_computation.3 | async-start | bytes 2359296 | tf_op jit(solution)/shard_map/while/body/eval_jaxpr/all_gather | solution.py:8
  753.6 54.6 %all-gather.17.cloned.1.call-start = ((), (), s32[]{:S(2)}) async-start(), calls=%async_computation.4 | async-start | bytes 2359296 | tf_op jit(solution)/shard_map/while/body/eval_jaxpr/all_gather | solution.py:8
  811.6 54.6 %all-gather.17.cloned.1.call-start = ((), (), s32[]{:S(2)}) async-start(), calls=%async_computation.4 | async-start | bytes 2359296 | tf_op jit(solution)/shard_map/while/body/eval_jaxpr/all_gather | solution.py:8
  869.5 54.7 %all-gather.17.cloned.1.call-start = ((), (), s32[]{:S(2)}) async-start(), calls=%async_computation.4 | async-start | bytes 2359296 | tf_op jit(solution)/shard_map/while/body/eval_jaxpr/all_gather | solution.py:8
  927.6 54.6 %all-gather.17.cloned.1.call-start = ((), (), s32[]{:S(2)}) async-start(), calls=%async_computation.4 | async-start | bytes 2359296 | tf_op jit(solution)/shard_map/while/body/eval_jaxpr/all_gather | solution.py:8
  985.5 54.6 %all-gather.17.cloned.1.call-start = ((), (), s32[]{:S(2)}) async-start(), calls=%async_computation.4 | async-start | bytes 2359296 | tf_op jit(solution)/shard_map/while/body/eval_jaxpr/all_gather | solution.py:8
  1043.5 54.6 %all-gather.17.cloned.1.call-start = ((), (), s32[]{:S(2)}) async-start(), calls=%async_computation.4 | async-start | bytes 2359296 | tf_op jit(solution)/shard_map/while/body/eval_jaxpr/all_gather | solution.py:8
  1101.5 54.6 %all-gather.17.cloned.1.call-start = ((), (), s32[]{:S(2)}) async-start(), calls=%async_computation.4 | async-start | bytes 2359296 | tf_op jit(solution)/shard_map/while/body/eval_jaxpr/all_gather | solution.py:8
  1159.5 54.6 %all-gather.17.cloned.1.call-start = ((), (), s32[]{:S(2)}) async-start(), calls=%async_computation.4 | async-start | bytes 2359296 | tf_op jit(solution)/shard_map/while/body/eval_jaxpr/all_gather | solution.py:8
  1217.5 0.8 copy-start
Sparse Core Ops, SparseCore 0:
  9.0 178.6 all-gather.12
  189.3 92.2 all-gather.10
  284.7 54.5 all-gather.14
  346.4 51.4 all-gather.14
  405.0 51.4 all-gather.14
  463.6 51.4 all-gather.14
  522.2 51.4 all-gather.14
  580.9 51.4 all-gather.14
  639.5 51.4 all-gather.14
  698.1 51.4 all-gather.14
  756.7 51.4 all-gather.16
  814.7 51.4 all-gather.16
  872.7 51.4 all-gather.16
  930.7 51.4 all-gather.16
  988.7 51.4 all-gather.16
  1046.7 51.4 all-gather.16
  1104.7 51.4 all-gather.16
  1162.7 51.4 all-gather.16
where the time goes:
time: 1230 us
  waiting for transfers between devices  1000 us (81%)
  matrix products  94.2 us (8%)
  other arithmetic  59.8 us (5%)
  local copies, waits for them, and re-layouts  45.9 us (4%)
  between operations  13.6 us (1%)
    all_gather x16, waiting for transfers between devices, picked(): lax.all_gather(array, axis)  814 us
    all_gather x1, waiting for transfers between devices, on_device(): lax.all_gather(tri_panels, 'col', axis=1, tiled=True)  91.5 us
    all_gather x1, waiting for transfers between devices, on_device(): lax.all_gather(own_inverse, 'col', axis=1, tiled=True)  82.4 us
    dot_general x16, matrix products, advance(): jnp.dot(inverse_block, current, precision=lax.Precision.HIGHEST, preferre...  46.7 us
    dot_general x16, matrix products, advance(): jnp.einsum('sij,jc->sic', pieces, solution, precision=lax.Precision.HIGHEST)  41.8 us
    another operation x4, other arithmetic, on_device(): jax.scipy.linalg.solve_triangular(own_diag, identity_block, lower=True)  41.5 us
  transfers between devices with their start and end apart: 19, of which 19 were waited for; matrix products, arithmetic and copies ran while one was open for 8% of the time, Pallas kernels for 0%

commit v1 on v0

--- a/solution.py
+++ b/solution.py
@@ -9,6 +9,12 @@
 
 
 def on_device(tri_panels, rhs_rows):
+
+    def see_the_sector(incoming_x, which_axis):
+        return jnp.concatenate(
+            lax.all_to_all(jnp.stack(lax.axis_size(which_axis) * [incoming_x]), which_axis, 0, 0), 1
+        )
+
     row_count = lax.axis_size("row")
     col_count = lax.axis_size("col")
     row_position = lax.axis_index("row")
@@ -51,7 +57,7 @@
 
     group_count = (col_count + row_count - 1) // row_count
     everything, inverses = (
-        lax.all_gather(tri_panels, "col", axis=1, tiled=True),
+        see_the_sector(tri_panels, "col"),
         lax.all_gather(own_inverse, "col", axis=1, tiled=True),
     )
     for first_slot in range(group_count):

time: 1230 us -> 1620 us (1.32)
  waiting for transfers between devices: 1000 us -> 1300 us
  local copies, waits for them, and re-layouts: 45.9 us -> 121 us
    all_to_all x0 -> x1, waiting for transfers between devices: none -> 484 us  [see_the_sector(): lax.all_to_all(jnp.stack(lax.axis_size(which_axis) * [incoming_x]), which...]
    all_gather x1 -> x0, waiting for transfers between devices: 91.5 us -> none  [on_device(): lax.all_gather(tri_panels, 'col', axis=1, tiled=True)]
    all_gather x1, waiting for transfers between devices: 82.4 us -> 0.01 us  [on_device(): lax.all_gather(own_inverse, 'col', axis=1, tiled=True)]
    all_to_all x0 -> x1, local copies, waits for them, and re-layouts: none -> 31.8 us  [see_the_sector(): lax.all_to_all(jnp.stack(lax.axis_size(which_axis) * [incoming_x]), which...]
    dynamic_slice x8 -> x16, local copies, waits for them, and re-layouts: 14.2 us -> 41.3 us  [upfront_step(): lax.dynamic_slice_in_dim(own_rows, step_index * block_size, block_size, 1)]
  transfers between devices with their start and end apart: 19 -> 19, of which waited for: 19 -> 17; matrix products, arithmetic and copies ran while one was open for 8% -> 10% of each run, Pallas kernels for 0% -> 0%
where the time goes in v1:
time: 1620 us; the launch traced here: 1610 us
  waiting for transfers between devices  1300 us (80%)
  local copies, waits for them, and re-layouts  121 us (7%)
  matrix products  103 us (6%)
  other arithmetic  61.6 us (4%)
    all_gather x16, waiting for transfers between devices, picked(): lax.all_gather(array, axis)  818 us
    all_to_all x1, waiting for transfers between devices, see_the_sector(): lax.all_to_all(jnp.stack(lax.axis_size(which_axis) * [incoming_x]), which...  484 us
    dot_general x16, matrix products, advance(): jnp.einsum('sij,jc->sic', pieces, solution, precision=lax.Precision.HIGHEST)  48.3 us
    dot_general x16, matrix products, advance(): jnp.dot(inverse_block, current, precision=lax.Precision.HIGHEST, preferre...  46.7 us
    another operation x4, other arithmetic, on_device(): jax.scipy.linalg.solve_triangular(own_diag, identity_block, lower=True)  42.3 us
    dynamic_slice x16, local copies, waits for them, and re-layouts, upfront_step(): lax.dynamic_slice_in_dim(own_rows, step_index * block_size, block_size, 1)  41.3 us
  transfers between devices with their start and end apart: 19, of which 17 were waited for; matrix products, arithmetic and copies ran while one was open for 10% of the time, Pallas kernels for 0%

profile of v1, /device:TPU:0, one launch (start us, length us, event | category | flops | bytes accessed | tf_op | source)
XLA Modules:
  0.0 1614.6 jit_solution(6475875258240399321)
XLA Ops:
  11.9 5.7 all-to-all-start
  19.9 14.4 while.33
  34.3 40.1 %custom-call.4 = f32[4,128,128]{1,2,0:T(8,128)S(1)} custom-call(f32[4,128,128]{2,1,0:T(8,128)} %get-tuple-element.290), custom_call_target="InvertDiagBlocksLowerTriangular" | custom-call | tf_op jit(solution)/shard_map/jit(_solve_triangular)/triangular_solve | solution.py:31
  82.9 11.3 stack.2
  94.2 6.0 all-to-all-start.1
  106.6 483.9 %all-to-all-done.1 = f32[16,1024,512]{2,1,0:T(8,128)} async-done(((f32[16,1024,512]{2,1,0:T(8,128)}), f32[16,1024,512]{2,1,0:T(8,128)}, u32[]{:S(2)}, u32[]{:S(2)}) %all-to-all-start.1) | async-done | bytes 33554464 | tf_op jit(solution)/shard_map/all_to_all | solution.py:15
  590.5 31.8 %copy.10 = f32[16,1024,512]{1,2,0:T(8,128)} copy(f32[16,1024,512]{2,1,0:T(8,128)} %all-to-all-done.1) | data formatting | bytes 67108864 | tf_op jit(solution)/shard_map/all_to_all | solution.py:15
  622.3 11.6 slice.74
  633.9 502.8 %while.31 = (s32[]{:T(128)}, f32[2,512,128]{2,1,0:T(8,128)S(1)}, s32[]{:T(128)}, f32[512,8192]{1,0:T(8,128)}, f32[1024,8192]{0,1:T(8,128)}, /*index=5*/s32[]{:T(...) while((s32[]{:T(128)}, f32[2,512,128]{2,1,0:T(8,128)S(1)}, ...), condition=%wide.region_1.2_spmd, body=%wide.region_0.1_spmd.sunk | while | flops 1208287232 | bytes 21234120 | solution.py:75
  636.9 3.2 constant_dynamic-slice_fusion.4
  642.0 80.4 %all-gather.12.cloned.1.call-done = f32[4096,128]{1,0:T(8,128)} async-done(((f32[512,128]{1,0:T(8,128)}), f32[4096,128]{1,0:T(8,128)}) %all-gather.12.cloned.1.call-update) | async-done | bytes 2097168 | tf_op jit(solution)/shard_map/while/body/eval_jaxpr/all_gather | solution.py:8
  723.5 3.0 fusion.64
  729.5 3.2 constant_dynamic-slice_fusion.4
  734.7 46.4 %all-gather.12.cloned.1.call-done = f32[4096,128]{1,0:T(8,128)} async-done(((f32[512,128]{1,0:T(8,128)}), f32[4096,128]{1,0:T(8,128)}) %all-gather.12.cloned.1.call-update) | async-done | bytes 2097168 | tf_op jit(solution)/shard_map/while/body/eval_jaxpr/all_gather | solution.py:8
  788.1 3.2 constant_dynamic-slice_fusion.4
  793.3 46.4 %all-gather.12.cloned.1.call-done = f32[4096,128]{1,0:T(8,128)} async-done(((f32[512,128]{1,0:T(8,128)}), f32[4096,128]{1,0:T(8,128)}) %all-gather.12.cloned.1.call-update) | async-done | bytes 2097168 | tf_op jit(solution)/shard_map/while/body/eval_jaxpr/all_gather | solution.py:8
  840.7 3.0 fusion.64
  846.7 3.2 constant_dynamic-slice_fusion.4
  851.9 46.4 %all-gather.12.cloned.1.call-done = f32[4096,128]{1,0:T(8,128)} async-done(((f32[512,128]{1,0:T(8,128)}), f32[4096,128]{1,0:T(8,128)}) %all-gather.12.cloned.1.call-update) | async-done | bytes 2097168 | tf_op jit(solution)/shard_map/while/body/eval_jaxpr/all_gather | solution.py:8
  899.3 3.0 fusion.64
  905.3 3.2 constant_dynamic-slice_fusion.4
  910.5 46.4 %all-gather.12.cloned.1.call-done = f32[4096,128]{1,0:T(8,128)} async-done(((f32[512,128]{1,0:T(8,128)}), f32[4096,128]{1,0:T(8,128)}) %all-gather.12.cloned.1.call-update) | async-done | bytes 2097168 | tf_op jit(solution)/shard_map/while/body/eval_jaxpr/all_gather | solution.py:8
  957.9 3.0 fusion.64
  963.9 3.2 constant_dynamic-slice_fusion.4
  969.1 46.4 %all-gather.12.cloned.1.call-done = f32[4096,128]{1,0:T(8,128)} async-done(((f32[512,128]{1,0:T(8,128)}), f32[4096,128]{1,0:T(8,128)}) %all-gather.12.cloned.1.call-update) | async-done | bytes 2097168 | tf_op jit(solution)/shard_map/while/body/eval_jaxpr/all_gather | solution.py:8
  1016.5 3.0 fusion.64
  1022.5 3.2 constant_dynamic-slice_fusion.4
  1027.7 46.4 %all-gather.12.cloned.1.call-done = f32[4096,128]{1,0:T(8,128)} async-done(((f32[512,128]{1,0:T(8,128)}), f32[4096,128]{1,0:T(8,128)}) %all-gather.12.cloned.1.call-update) | async-done | bytes 2097168 | tf_op jit(solution)/shard_map/while/body/eval_jaxpr/all_gather | solution.py:8
  1075.2 3.0 fusion.64
  1081.2 3.2 constant_dynamic-slice_fusion.4
  1086.3 46.4 %all-gather.12.cloned.1.call-done = f32[4096,128]{1,0:T(8,128)} async-done(((f32[512,128]{1,0:T(8,128)}), f32[4096,128]{1,0:T(8,128)}) %all-gather.12.cloned.1.call-update) | async-done | bytes 2097168 | tf_op jit(solution)/shard_map/while/body/eval_jaxpr/all_gather | solution.py:8
  1136.7 470.5 %while.32 = (s32[]{:T(128)}, f32[2,512,128]{2,1,0:T(8,128)S(1)}, s32[]{:T(128)}, f32[512,8192]{1,0:T(8,128)}, s32[1]{0:T(128)}, /*index=5*/f32[512,8192]{0,1:T(8...) while((s32[]{:T(128)}, f32[2,512,128]{2,1,0:T(8,128)S(1)}, ...), condition=%wide.region_3.4_spmd, body=%wide.region_2.3_spmd.sunk | while | flops 805634048 | bytes 12846105 | solution.py:75
  1139.8 51.6 %all-gather.14.cloned.1.call-done = f32[4096,128]{1,0:T(8,128)} async-done(((f32[512,128]{1,0:T(8,128)}), f32[4096,128]{1,0:T(8,128)}) %all-gather.14.cloned.1.call-update) | async-done | bytes 2097168 | tf_op jit(solution)/shard_map/while/body/eval_jaxpr/all_gather | solution.py:8
  1192.4 3.1 fusion.70
  1198.6 51.6 %all-gather.14.cloned.1.call-done = f32[4096,128]{1,0:T(8,128)} async-done(((f32[512,128]{1,0:T(8,128)}), f32[4096,128]{1,0:T(8,128)}) %all-gather.14.cloned.1.call-update) | async-done | bytes 2097168 | tf_op jit(solution)/shard_map/while/body/eval_jaxpr/all_gather | solution.py:8
  1251.2 3.1 fusion.70
  1257.5 51.6 %all-gather.14.cloned.1.call-done = f32[4096,128]{1,0:T(8,128)} async-done(((f32[512,128]{1,0:T(8,128)}), f32[4096,128]{1,0:T(8,128)}) %all-gather.14.cloned.1.call-update) | async-done | bytes 2097168 | tf_op jit(solution)/shard_map/while/body/eval_jaxpr/all_gather | solution.py:8
  1310.1 3.1 fusion.70
  1316.3 51.6 %all-gather.14.cloned.1.call-done = f32[4096,128]{1,0:T(8,128)} async-done(((f32[512,128]{1,0:T(8,128)}), f32[4096,128]{1,0:T(8,128)}) %all-gather.14.cloned.1.call-update) | async-done | bytes 2097168 | tf_op jit(solution)/shard_map/while/body/eval_jaxpr/all_gather | solution.py:8
  1368.9 3.1 fusion.70
  1375.1 51.6 %all-gather.14.cloned.1.call-done = f32[4096,128]{1,0:T(8,128)} async-done(((f32[512,128]{1,0:T(8,128)}), f32[4096,128]{1,0:T(8,128)}) %all-gather.14.cloned.1.call-update) | async-done | bytes 2097168 | tf_op jit(solution)/shard_map/while/body/eval_jaxpr/all_gather | solution.py:8
  1427.7 3.1 fusion.70
  1433.9 51.6 %all-gather.14.cloned.1.call-done = f32[4096,128]{1,0:T(8,128)} async-done(((f32[512,128]{1,0:T(8,128)}), f32[4096,128]{1,0:T(8,128)}) %all-gather.14.cloned.1.call-update) | async-done | bytes 2097168 | tf_op jit(solution)/shard_map/while/body/eval_jaxpr/all_gather | solution.py:8
  1486.5 3.1 fusion.70
  1492.7 51.6 %all-gather.14.cloned.1.call-done = f32[4096,128]{1,0:T(8,128)} async-done(((f32[512,128]{1,0:T(8,128)}), f32[4096,128]{1,0:T(8,128)}) %all-gather.14.cloned.1.call-update) | async-done | bytes 2097168 | tf_op jit(solution)/shard_map/while/body/eval_jaxpr/all_gather | solution.py:8
  1545.3 3.1 fusion.70
  1551.5 51.6 %all-gather.14.cloned.1.call-done = f32[4096,128]{1,0:T(8,128)} async-done(((f32[512,128]{1,0:T(8,128)}), f32[4096,128]{1,0:T(8,128)}) %all-gather.14.cloned.1.call-update) | async-done | bytes 2097168 | tf_op jit(solution)/shard_map/while/body/eval_jaxpr/all_gather | solution.py:8
  1604.1 3.1 fusion.70
  (144 shorter events, 122.8 us)
Async XLA Ops:
  11.9 6.9 copy-start.1
  11.9 71.0 %all-to-all-start = ((f32[16,1,8192]{2,1,0:T(1,128)}), f32[16,1,8192]{2,1,0:T(1,128)S(1)}, u32[]{:S(2)}, u32[]{:S(2)}) async-start(f32[16,1,8192]{2,1,0:T(1,128)} %reshape.94), calls=%async_computation | async-start | bytes 1048576 | tf_op jit(solution)/shard_map/all_to_all | solution.py:26
  74.5 0.7 copy-start.3
  75.5 4.1 copy-start.4
  94.2 6.3 copy-start.2
  94.2 496.3 %all-to-all-start.1 = ((f32[16,1024,512]{2,1,0:T(8,128)}), f32[16,1024,512]{2,1,0:T(8,128)}, u32[]{:S(2)}, u32[]{:S(2)}) async-start(f32[16,1024,512]{2,1,0:T(8,128)} %stack.2), calls=%async_computation.1 | async-start | bytes 67108864 | tf_op jit(solution)/shard_map/all_to_all | solution.py:15
  100.3 533.6 %all-gather.10.cloned.1.call-start = ((), (), s32[]{:S(2)}) async-start(), calls=%async_computation.2 | async-start | bytes 17825792 | tf_op jit(solution)/shard_map/all_gather | solution.py:61
  633.9 88.6 %all-gather.12.cloned.1.call-start = ((), (), s32[]{:S(2)}) async-start(), calls=%async_computation.3 | async-start | bytes 2359296 | tf_op jit(solution)/shard_map/while/body/eval_jaxpr/all_gather | solution.py:8
  726.5 54.6 %all-gather.12.cloned.1.call-start = ((), (), s32[]{:S(2)}) async-start(), calls=%async_computation.3 | async-start | bytes 2359296 | tf_op jit(solution)/shard_map/while/body/eval_jaxpr/all_gather | solution.py:8
  785.1 54.6 %all-gather.12.cloned.1.call-start = ((), (), s32[]{:S(2)}) async-start(), calls=%async_computation.3 | async-start | bytes 2359296 | tf_op jit(solution)/shard_map/while/body/eval_jaxpr/all_gather | solution.py:8
  843.7 54.6 %all-gather.12.cloned.1.call-start = ((), (), s32[]{:S(2)}) async-start(), calls=%async_computation.3 | async-start | bytes 2359296 | tf_op jit(solution)/shard_map/while/body/eval_jaxpr/all_gather | solution.py:8
  902.3 54.6 %all-gather.12.cloned.1.call-start = ((), (), s32[]{:S(2)}) async-start(), calls=%async_computation.3 | async-start | bytes 2359296 | tf_op jit(solution)/shard_map/while/body/eval_jaxpr/all_gather | solution.py:8
  960.9 54.7 %all-gather.12.cloned.1.call-start = ((), (), s32[]{:S(2)}) async-start(), calls=%async_computation.3 | async-start | bytes 2359296 | tf_op jit(solution)/shard_map/while/body/eval_jaxpr/all_gather | solution.py:8
  1019.5 54.6 %all-gather.12.cloned.1.call-start = ((), (), s32[]{:S(2)}) async-start(), calls=%async_computation.3 | async-start | bytes 2359296 | tf_op jit(solution)/shard_map/while/body/eval_jaxpr/all_gather | solution.py:8
  1078.1 54.6 %all-gather.12.cloned.1.call-start = ((), (), s32[]{:S(2)}) async-start(), calls=%async_computation.3 | async-start | bytes 2359296 | tf_op jit(solution)/shard_map/while/body/eval_jaxpr/all_gather | solution.py:8
  1136.8 54.6 %all-gather.14.cloned.1.call-start = ((), (), s32[]{:S(2)}) async-start(), calls=%async_computation.4 | async-start | bytes 2359296 | tf_op jit(solution)/shard_map/while/body/eval_jaxpr/all_gather | solution.py:8
  1195.6 54.6 %all-gather.14.cloned.1.call-start = ((), (), s32[]{:S(2)}) async-start(), calls=%async_computation.4 | async-start | bytes 2359296 | tf_op jit(solution)/shard_map/while/body/eval_jaxpr/all_gather | solution.py:8
  1254.4 54.6 %all-gather.14.cloned.1.call-start = ((), (), s32[]{:S(2)}) async-start(), calls=%async_computation.4 | async-start | bytes 2359296 | tf_op jit(solution)/shard_map/while/body/eval_jaxpr/all_gather | solution.py:8
  1313.2 54.7 %all-gather.14.cloned.1.call-start = ((), (), s32[]{:S(2)}) async-start(), calls=%async_computation.4 | async-start | bytes 2359296 | tf_op jit(solution)/shard_map/while/body/eval_jaxpr/all_gather | solution.py:8
  1372.0 54.6 %all-gather.14.cloned.1.call-start = ((), (), s32[]{:S(2)}) async-start(), calls=%async_computation.4 | async-start | bytes 2359296 | tf_op jit(solution)/shard_map/while/body/eval_jaxpr/all_gather | solution.py:8
  1430.8 54.6 %all-gather.14.cloned.1.call-start = ((), (), s32[]{:S(2)}) async-start(), calls=%async_computation.4 | async-start | bytes 2359296 | tf_op jit(solution)/shard_map/while/body/eval_jaxpr/all_gather | solution.py:8
  1489.7 54.6 %all-gather.14.cloned.1.call-start = ((), (), s32[]{:S(2)}) async-start(), calls=%async_computation.4 | async-start | bytes 2359296 | tf_op jit(solution)/shard_map/while/body/eval_jaxpr/all_gather | solution.py:8
  1548.5 54.6 %all-gather.14.cloned.1.call-start = ((), (), s32[]{:S(2)}) async-start(), calls=%async_computation.4 | async-start | bytes 2359296 | tf_op jit(solution)/shard_map/while/body/eval_jaxpr/all_gather | solution.py:8
  1607.3 0.8 copy-start
Sparse Core Ops, SparseCore 0:
  102.7 440.4 all-gather.9
  637.1 85.3 all-gather.11
  729.6 51.4 all-gather.11
  788.2 51.4 all-gather.11
  846.8 51.4 all-gather.11
  905.4 51.4 all-gather.11
  964.0 51.4 all-gather.11
  1022.7 51.4 all-gather.11
  1081.3 51.4 all-gather.11
  1139.9 51.4 all-gather.13
  1198.7 51.4 all-gather.13
  1257.6 51.4 all-gather.13
  1316.4 51.4 all-gather.13
  1375.2 51.4 all-gather.13
  1434.0 51.4 all-gather.13
  1492.8 51.4 all-gather.13
  1551.6 51.4 all-gather.13
